TPU v7x, 32 devices: a whole 2x2x4 slice. The times are simulated.
32 devices in a mesh: dp: 16 (over z, y, x), mp: 2 (over core).
Axes of the slice: x: 2, y: 2, z: 4, core: 2. Of those that a mesh axis runs over, the one named last changes fastest.
Arguments:
- hidden: bfloat16 [240, 128, 2048], P('dp', None, 'mp'), may hold values from -6 to 6
- attn_out: bfloat16 [240, 128, 2048], P('dp', None, 'mp'), may hold values from -6 to 6
- out_proj: bfloat16 [2048, 2048], P(None, 'mp'), may hold values from -0.125 to 0.125
- norm_gain: float32 [2048], P('mp'), may hold values from 0.1 to 1.9
- reward_proj: float32 [2048, 8], P('mp'), may hold values from -0.125 to 0.125
- block_seq: int32 [240], replicated, may hold values from -1 to 95, as said below
- block_dest: int32 [240], replicated, may hold values from -1 to 159, as said below
- lengths: int32 [96], replicated, may hold values from 1 to 512, as said below
Outputs:
- token_rewards: float32 [160, 8, 128], P('dp')
- advantages: float32 [96], P('dp')
Inputs may be any that keep to these rules, and one draw needn't show every extreme that they name: `block_seq`: used slots of each index of dp come first in its 15 slots, the rest hold -1; each index of dp holds 1 to 15 used slots and some index holds exactly 15. Read over used slots in slot order, response numbers never fall, every response appears, and each has 1 to 4 blocks. `block_dest`: exactly the used slots (those of block_seq that are not -1) hold a destination; every owned slot of every owner is named exactly once, so each owner receives exactly 10 blocks; at most 1 block go from one index of dp to one owner, and that many in some pair. `lengths`: A response of n blocks has more than 128 * (n - 1) and at most 128 * n tokens.
All inputs are finite; a program needn't handle non-finite values.
Results may differ from a plain program's by a relative error of at most 0.0029.
Values may be sent and summed in bfloat16 or wider, within the bound.
A program may use at most 64 MiB of HBM per device.

v0:
```python
import jax
import jax.numpy as jnp
from jax import lax
from jax.sharding import PartitionSpec as P

OWN_CAP = 10


norm_epsilon = 1e-05
stat_epsilon = 1e-06


def local(hidden, attn_out, out_proj, norm_gain, reward_proj, block_seq, block_dest, lengths):
    device_count = lax.axis_size("dp")
    device_rank = lax.axis_index("dp")
    slots_in = hidden.shape[0]
    block_len = hidden.shape[1]
    model_width = out_proj.shape[0]
    seq_count = lengths.shape[0]
    seq_local = seq_count // device_count
    slot_depth = (slots_in + device_count - 1) // device_count
    all_slots = jnp.arange(block_dest.shape[0], dtype=jnp.int32)
    local_dest = lax.dynamic_slice_in_dim(block_dest, device_rank * slots_in, slots_in)
    is_used = local_dest >= 0
    owner_rank = jnp.where(is_used, local_dest // OWN_CAP, -1)
    local_slots = jnp.arange(slots_in, dtype=jnp.int32)
    earlier = (
        (owner_rank[None, :] == owner_rank[:, None])
        & (local_slots[None, :] < local_slots[:, None])
        & is_used[None, :]
    )
    send_row = jnp.where(is_used, owner_rank * slot_depth + earlier.sum(axis=1), -1)
    buffer_rows = jnp.arange(device_count * slot_depth, dtype=jnp.int32)
    selector = (send_row[None, :] == buffer_rows[:, None]).astype(jnp.bfloat16)
    targets = device_rank * OWN_CAP + jnp.arange(OWN_CAP, dtype=jnp.int32)
    matches = block_dest[None, :] == targets[:, None]
    source_slot = jnp.sum(jnp.where(matches, all_slots[None, :], 0), axis=1)
    source_rank = source_slot // slots_in
    before = (block_dest[None, :] >= 0) & (block_dest[None, :] // OWN_CAP == device_rank)
    before = (
        before
        & (all_slots[None, :] >= (source_rank * slots_in)[:, None])
        & (all_slots[None, :] < source_slot[:, None])
    )
    recv_row = source_rank * slot_depth + before.sum(axis=1)
    seq_own = jnp.sum(jnp.where(matches, block_seq[None, :], 0), axis=1)
    earlier_same = (block_seq[None, :] == seq_own[:, None]) & (
        all_slots[None, :] < source_slot[:, None]
    )
    seq_rank = earlier_same.sum(axis=1)
    seq_ids = jnp.arange(seq_count, dtype=jnp.int32)
    member = seq_ids[:, None] == seq_own[None, :]
    own_length = jnp.sum(jnp.where(member, lengths[:, None], 0), axis=0)
    valid_tokens = jnp.minimum(block_len, own_length - block_len * seq_rank)
    projected = jnp.einsum(
        "btf,fc->btc",
        lax.all_gather(attn_out, "mp", axis=2, tiled=True),
        out_proj,
        preferred_element_type=jnp.float32,
    )
    local_resid = (hidden.astype(jnp.float32) + projected).astype(jnp.bfloat16)
    moved_resid = lax.all_to_all(
        jnp.einsum("rj,jtf->rtf", selector, local_resid, preferred_element_type=jnp.float32).astype(
            jnp.bfloat16
        ),
        "dp",
        split_axis=0,
        concat_axis=0,
        tiled=True,
    )
    residual = jnp.take(moved_resid, recv_row, axis=0)
    values = residual.astype(jnp.float32)
    squares = jnp.sum(values * values, axis=2)
    weighted = norm_gain[:, None] * reward_proj
    partial_value = jnp.einsum("btf,fh->bht", values, weighted, precision=lax.Precision.HIGHEST)
    squares, partial_value = lax.psum((squares, partial_value), "mp")
    inverse_rms = lax.rsqrt(squares / model_width + norm_epsilon)
    live_tokens = (jnp.arange(block_len, dtype=jnp.int32)[None, :] < valid_tokens[:, None]).astype(
        jnp.float32
    )
    token_rewards = partial_value * (inverse_rms * live_tokens)[:, None, :]
    block_sums = jnp.sum(token_rewards, axis=2)
    seq_part = jnp.dot(member.astype(jnp.float32), block_sums, precision=lax.Precision.HIGHEST)
    seq_totals = lax.psum_scatter(seq_part, "dp", scatter_dimension=0, tiled=True)
    own_lengths = lax.dynamic_slice_in_dim(lengths, device_rank * seq_local, seq_local).astype(
        jnp.float32
    )
    scores = seq_totals / own_lengths[:, None]
    worst_case = jnp.min(scores, axis=1)
    head_mean = jnp.mean(scores, axis=1)
    spread = jnp.mean((scores - head_mean[:, None]) ** 2, axis=1)
    total_seqs = float(seq_count)
    moment_sums = lax.psum(
        (
            jnp.sum(spread),
            jnp.sum(worst_case),
            jnp.sum(worst_case * worst_case),
            jnp.sum(worst_case * spread),
            jnp.sum(spread * spread),
        ),
        "dp",
    )
    penalty_scale = moment_sums[0] / total_seqs + stat_epsilon
    conservative = worst_case - spread / penalty_scale
    first_sum = moment_sums[1] - moment_sums[0] / penalty_scale
    second = (
        moment_sums[2]
        - 2.0 * moment_sums[3] / penalty_scale
        + moment_sums[4] / (penalty_scale * penalty_scale)
    )
    centre = first_sum / total_seqs
    variance = second / total_seqs - centre * centre
    advantages = (conservative - centre) * lax.rsqrt(variance + stat_epsilon)
    return (token_rewards, advantages)


def solution(mesh):
    return jax.shard_map(
        local,
        mesh=mesh,
        in_specs=(
            P("dp", None, "mp"),
            P("dp", None, "mp"),
            P(None, "mp"),
            P("mp"),
            P("mp", None),
            P(),
            P(),
            P(),
        ),
        out_specs=(P("dp", None, None), P("dp")),
        check_vma=False,
    )
```

profile of v0, /device:TPU:0, one launch (start us, length us, event | category | flops | bytes accessed | tf_op | source)
XLA Modules:
  0.0 287.4 jit_solution(6346611009013374957)
XLA Ops:
  7.2 0.0 all-gather.2.cloned.1.call-start
  7.2 0.7 all-gather.2.cloned.1.call-update
  7.9 0.8 fusion.26
  8.7 0.2 convert_reduce_fusion.2
  8.9 22.5 %all-gather.2.cloned.1.call-done = bf16[15,128,2048]{2,1,0:T(8,128)(2,1)} async-done(((bf16[15,128,1024]{2,1,0:T(8,128)(2,1)}), bf16[15,128,2048]{2,1,0:T(8,128)(2,1)}) %all-gather.2.cloned.1.call-update) | async-done | bytes 7864336 | tf_op jit(solution)/shard_map/all_gather | solution.py:57
  31.4 12.5 %add_convert_fusion = bf16[15,128,1024]{2,1,0:T(8,128)(2,1)S(1)} fusion(bf16[15,128,1024]{2,1,0:T(8,128)(2,1)} %param.8, bf16[15,128,2048]{2,1,0:T(8,128)(2,1)} %all-gather.2.cloned.1.call-done, bf16[2048,1024]{1,0:T(8,128)(2,1)} %param.10), kind=kOutput, calls=%fused_computation.1 | convolution fusion | flops 8058961920 | bytes 19922944 | tf_op jit(solution)/shard_map/btf,fc->btc/dot_general | solution.py:55
  43.8 2.8 fusion.4
  46.6 4.3 %copy.17 = bf16[16,128,1024]{2,1,0:T(8,128)(2,1)} copy(bf16[16,128,1024]{2,0,1:T(8,128)(2,1)S(1)} %fusion.4) | data formatting | bytes 8388608 | tf_op jit(solution)/shard_map/convert_element_type | solution.py:63
  50.9 0.0 copy-start.5
  50.9 0.0 copy-start.4
  50.9 0.0 copy-start
  50.9 0.0 copy-start.1
  50.9 7.0 %all-to-all-start = ((bf16[16,128,1024]{2,1,0:T(8,128)(2,1)}), bf16[16,128,1024]{2,1,0:T(8,128)(2,1)}, u32[]{:S(2)}, u32[]{:S(2)}) async-start(bf16[16,128,1024]{2,1,0:T(8,128)(2,1)} %copy.17), calls=%async_computation | async-start | bytes 8388608 | tf_op jit(solution)/shard_map/all_to_all | solution.py:62
  57.9 0.0 copy-start.2
  57.9 0.0 copy-start.3
  58.0 0.0 copy-done.5
  58.0 0.6 dynamic-slice
  59.2 0.0 copy-done.4
  59.2 0.1 dynamic-slice_convert_fusion
  59.3 0.0 copy-done
  59.3 0.0 copy-done.1
  59.3 0.2 fusion.12
  59.5 0.2 convert_reduce_fusion
  59.8 0.2 select_reduce_fusion
  60.0 78.5 %all-to-all-done = bf16[16,128,1024]{2,1,0:T(8,128)(2,1)} async-done(((bf16[16,128,1024]{2,1,0:T(8,128)(2,1)}), bf16[16,128,1024]{2,1,0:T(8,128)(2,1)}, u32[]{:S(2)}, u32[]{:S(2)}) %all-to-all-start) | async-done | bytes 4194336 | tf_op jit(solution)/shard_map/all_to_all | solution.py:62
  138.4 2.9 %gather_fusion = bf16[10,128,1024]{2,1,0:T(8,128)(2,1)S(1)} fusion(bf16[16,128,1024]{2,1,0:T(8,128)(2,1)} %all-to-all-done, s32[1024]{0:T(1024)S(1)} %pad_clamp_fusion), kind=kCustom, calls=%fused_computation | custom fusion | bytes 5242920 | tf_op jit(solution)/shard_map/jit(_take)/gather | solution.py:71
  141.3 0.8 multiply_reduce_fusion
  142.1 0.0 copy-done.2
  142.2 0.0 copy-done.3
  142.2 2.2 convolution_bitcast_fusion
  144.4 3.6 %all-reduce.2 = (f32[10,8,128]{2,1,0:T(8,128)S(1)}, f32[10,128]{1,0:T(8,128)S(1)}) all-reduce(f32[10,8,128]{2,1,0:T(8,128)S(1)} %convolution_bitcast_fusion, f32[10,128]{1,0:T(8,128)S(1)} %multiply_reduce_fusion), channel_id=1, replica_groups=mesh['dp'=16,'mp'=2] {'mp'}, use_global_device_ids=true, to_apply=%region_3.4 | all-reduce | flops 11520 | bytes 92160 | tf_op jit(solution)/shard_map/psum | solution.py:76
  147.9 0.1 rsqrt_select_fusion
  148.0 0.6 fusion.31
  148.6 0.3 fusion.17
  148.9 89.0 %all-reduce = f32[96,8]{1,0:T(8,128)S(1)} all-reduce(f32[96,8]{1,0:T(8,128)S(1)} %fusion.17), channel_id=2, replica_groups=mesh['dp'=16,'mp'=2] {'dp'}, use_global_device_ids=true, to_apply=%region_10.11.clone | all-reduce | flops 768 | bytes 6144
  237.9 0.2 fusion.30
  238.1 0.2 multiply_reduce_fusion.1
  238.3 0.7 fusion.29
  239.0 37.3 %all-reduce.1 = (f32[]{:T(128)}, f32[]{:T(128)}, f32[]{:T(128)}, f32[]{:T(128)}, f32[]{:T(128)}) all-reduce(f32[]{:T(128)} %get-tuple-element.10, f32[]{:T(128)} %get-tuple-element.7, f32[]{:T(128)} %get-tuple-element.9, f32[]{:T(128)} %get-tuple-element.8, f32[]{:T(128)} %get-tuple-element.6), channel_id=1, replica_groups=mesh['dp'=16,'mp'=2] {'dp'}, use_global_device_ids=true, to_apply=%region_19.20 | all-reduce | flops 5 | bytes 40 | tf_op jit(solution)/shard_map/psum | solution.py:93
  280.1 0.5 subtract_multiply_fusion
  (9 shorter events, 0.1 us)
Async XLA Ops:
  7.2 24.2 %all-gather.2.cloned.1.call-start = ((), (), s32[]{:S(2)}) async-start(), calls=%async_computation.1 | async-start | bytes 11796480 | tf_op jit(solution)/shard_map/all_gather | solution.py:57
  50.9 7.0 %copy-start.5 = (u32[32]{0:T(128)S(1)}, u32[32]{0:T(128)}, u32[]{:S(2)}) copy-start(u32[32]{0:T(128)} %constant.86) | copy-start | bytes 388
  50.9 8.3 %copy-start.4 = (s32[96]{0:T(128)S(1)}, s32[96]{0:T(128)}, u32[]{:S(2)}) copy-start(s32[96]{0:T(128)} %param.15) | copy-start | bytes 1156
  50.9 8.4 %copy-start = (s32[240]{0:T(256)S(1)}, s32[240]{0:T(256)}, u32[]{:S(2)}) copy-start(s32[240]{0:T(256)} %param.14) | copy-start | bytes 2884
  50.9 8.4 %copy-start.1 = (s32[240]{0:T(256)S(1)}, s32[240]{0:T(256)}, u32[]{:S(2)}) copy-start(s32[240]{0:T(256)} %param.13) | copy-start | bytes 2884
  50.9 87.5 %all-to-all-start = ((bf16[16,128,1024]{2,1,0:T(8,128)(2,1)}), bf16[16,128,1024]{2,1,0:T(8,128)(2,1)}, u32[]{:S(2)}, u32[]{:S(2)}) async-start(bf16[16,128,1024]{2,1,0:T(8,128)(2,1)} %copy.17), calls=%async_computation | async-start | bytes 8388608 | tf_op jit(solution)/shard_map/all_to_all | solution.py:62
  57.9 84.2 %copy-start.2 = (f32[1024,8]{0,1:T(8,128)S(1)}, f32[1024,8]{0,1:T(8,128)}, u32[]{:S(2)}) copy-start(f32[1024,8]{0,1:T(8,128)} %param.12) | copy-start | bytes 98308
  57.9 84.2 %copy-start.3 = (f32[1024]{0:T(1024)S(1)}, f32[1024]{0:T(1024)}, u32[]{:S(2)}) copy-start(f32[1024]{0:T(1024)} %param.11) | copy-start | bytes 12292
Sparse Core Ops, SparseCore 0:
  9.5 21.7 all-gather.1
where the time goes:
time: 288 us; the launch traced here: 287 us
  blocking collectives  130 us (45%)
  waiting for transfers between devices  102 us (35%)
  between operations  18.6 us (6%)
  matrix products  17.7 us (6%)
  local copies, waits for them, and re-layouts  7.81 us (3%)
  starting transfers between devices  7.03 us (2%)
  other arithmetic  4.79 us (2%)
    unnamed x1, blocking collectives  89 us
    all_to_all x1, waiting for transfers between devices, local(): lax.all_to_all(jnp.einsum('rj,jtf->rtf', selector, local_resid, preferred...  78.5 us
    psum x1, blocking collectives, local(): lax.psum((jnp.sum(spread), jnp.sum(worst_case), jnp.sum(worst_case * wors...  37.3 us
    all_gather x1, waiting for transfers between devices, local(): lax.all_gather(attn_out, 'mp', axis=2, tiled=True)  22.5 us
    dot_general x1, matrix products, local(): jnp.einsum('btf,fc->btc', lax.all_gather(attn_out, 'mp', axis=2, tiled=Tr...  12.5 us
    all_to_all x1, starting transfers between devices, local(): lax.all_to_all(jnp.einsum('rj,jtf->rtf', selector, local_resid, preferred...  6.99 us
  transfers between devices with their start and end apart: 2, of which 2 were waited for; matrix products, arithmetic and copies ran while one was open for 1% of the time, Pallas kernels for 0%

commit v1 on v0

v1 whole, which is shorter than its diff:
```python
import functools

import jax
import jax.numpy as jnp
from jax import lax
from jax.experimental import pallas as pl
from jax.experimental.pallas import tpu as pltpu
from jax.sharding import PartitionSpec as P

OWN_CAP = 10

norm_epsilon = 1e-05
stat_epsilon = 1e-06
MESH = pl.DeviceIdType.MESH
LANES = 128


def split_size(slots):
    for size in (3, 4, 2, 5):
        if slots % size == 0:
            return size
    return 1


def kernel(
    n_dp, n_mp, slots, block_len, seq_count, per_group,
    hidden_hbm, attn_hbm, w_hbm, gain_ref, reward_ref, seq_s, dest_s, len_s, seq_v, dest_v, len_v,
    rewards_out, adv_out,
    attn, w, hidden, acc, resid, heads_w, part, live, rewards, seq_acc, send_buf, recv_buf, adv_buf,
    send_idx, recv_idx,
    w_sem, own_sem, hid_sem, attn_send, attn_recv, part_send, part_recv, dp_send, dp_recv,
):
    dp = lax.axis_index("dp")
    mp = lax.axis_index("mp")
    groups = slots // per_group
    rows = per_group * block_len
    k_local = attn_hbm.shape[1]
    n_local = w_hbm.shape[1]
    model_width = w_hbm.shape[0]
    chunk = min(256, n_local)
    n_chunks = n_local // chunk

    barrier = pltpu.get_barrier_semaphore()
    for off in range(1, n_mp):
        pl.semaphore_signal(barrier, inc=1, device_id=(dp, lax.rem(mp + off, n_mp)), device_id_type=MESH)
    for off in range(1, n_dp):
        pl.semaphore_signal(barrier, inc=1, device_id=(lax.rem(dp + off, n_dp), mp), device_id_type=MESH)

    def w_copy(m):
        start = pl.multiple_of(m * k_local, k_local)
        return pltpu.make_async_copy(w_hbm.at[pl.ds(start, k_local)], w.at[m], w_sem.at[m])

    def group_rows(g):
        return pl.ds(pl.multiple_of(g * rows, rows), rows)

    def own_copy(g):
        return pltpu.make_async_copy(attn_hbm.at[group_rows(g)], attn.at[mp, group_rows(g)], own_sem.at[g])

    def hid_copy(g):
        return pltpu.make_async_copy(hidden_hbm.at[group_rows(g)], hidden.at[group_rows(g)], hid_sem.at[g])

    def attn_copy(off, g):
        return pltpu.make_async_remote_copy(
            src_ref=attn_hbm.at[group_rows(g)],
            dst_ref=attn.at[mp, group_rows(g)],
            send_sem=attn_send.at[off - 1, g],
            recv_sem=attn_recv.at[off - 1, g],
            device_id=(dp, lax.rem(mp + off, n_mp)),
            device_id_type=MESH,
        )

    def part_copy(off, g):
        return pltpu.make_async_remote_copy(
            src_ref=part.at[mp, g],
            dst_ref=part.at[mp, g],
            send_sem=part_send.at[off - 1, g],
            recv_sem=part_recv.at[off - 1, g],
            device_id=(dp, lax.rem(mp + off, n_mp)),
            device_id_type=MESH,
        )

    def dp_copy(off):
        peer = lax.rem(dp + off, n_dp)
        return pltpu.make_async_remote_copy(
            src_ref=send_buf.at[peer],
            dst_ref=recv_buf.at[dp],
            send_sem=dp_send.at[off - 1],
            recv_sem=dp_recv.at[off - 1],
            device_id=(peer, mp),
            device_id_type=MESH,
        )

    w_copy(mp).start()
    for g in range(groups):
        own_copy(g).start()
    for off in range(1, n_mp):
        w_copy(lax.rem(mp + off, n_mp)).start()
    for g in range(groups):
        hid_copy(g).start()

    head_count = reward_ref.shape[0]
    weighted = reward_ref[...] * gain_ref[...].reshape(1, n_local)
    high = weighted.astype(jnp.bfloat16)
    rest = weighted - high.astype(jnp.float32)
    middle = rest.astype(jnp.bfloat16)
    low = (rest - middle.astype(jnp.float32)).astype(jnp.bfloat16)
    heads_w[...] = jnp.concatenate([high, middle, low, jnp.zeros_like(low)], axis=0)

    base = dp * slots

    def send_body(r, carry):
        low_dest = r * OWN_CAP
        found = jnp.int32(0)
        for j in range(slots):
            d = dest_s[base + j]
            found = jnp.where((d >= low_dest) & (d < low_dest + OWN_CAP), jnp.int32(j), found)
        send_idx[r] = found
        return carry

    lax.fori_loop(0, n_dp, send_body, 0)
    all_slots = seq_s.shape[0]
    slot_lane = lax.broadcasted_iota(jnp.int32, (1, all_slots), 1)
    dest_row = dest_v[...].reshape(1, all_slots)
    seq_row = seq_v[...].reshape(1, all_slots)
    for q in range(OWN_CAP):
        place = jnp.max(jnp.where(dest_row == dp * OWN_CAP + q, slot_lane, 0))
        recv_idx[q] = lax.div(place, slots)
    token = lax.broadcasted_iota(jnp.int32, (1, block_len), 1).astype(jnp.float32)
    for j in range(slots):
        seq = seq_s[base + j]
        earlier = jnp.where((seq_row == seq) & (slot_lane < base + j), 1.0, 0.0)
        rank = jnp.sum(earlier, axis=1, keepdims=True)
        length = len_s[jnp.maximum(seq, 0)].astype(jnp.float32)
        valid = length - rank * float(block_len)
        live[j : j + 1, :] = jnp.where(token < valid, 1.0, 0.0)
    seq_acc[...] = jnp.zeros_like(seq_acc)

    pl.semaphore_wait(barrier, n_mp - 1 + n_dp - 1)
    for g in range(groups):
        for off in range(1, n_mp):
            attn_copy(off, g).start()

    w_copy(mp).wait()

    def first_half(g, carry):
        own_copy(g).wait()
        for c in range(n_chunks):
            cols = slice(c * chunk, (c + 1) * chunk)
            acc[group_rows(g), cols] = jnp.dot(
                attn[mp, group_rows(g), :], w[mp, :, cols], preferred_element_type=jnp.float32
            )
        return carry

    lax.fori_loop(0, groups, first_half, 0)
    for off in range(1, n_mp):
        w_copy(lax.rem(mp + off, n_mp)).wait()

    seq_lane = lax.broadcasted_iota(jnp.int32, (head_count, seq_acc.shape[1]), 1)

    def finish(g):
        for off in range(1, n_mp):
            part_copy(off, g).wait()
        total = part[0, g]
        for m in range(1, n_mp):
            total = total + part[m, g]
        scale = lax.rsqrt(total[head_count:] / model_width + norm_epsilon)
        values = total[:head_count] * scale
        for b in range(per_group):
            j = g * per_group + b
            block = values[:, b * block_len : (b + 1) * block_len] * live[pl.ds(j, 1), :]
            rewards[j] = block
            sums = jnp.sum(block, axis=1, keepdims=True)
            seq_acc[...] += jnp.where(seq_lane == seq_s[base + j], sums, 0.0)

    def second_half(g, carry):
        hid_copy(g).wait()
        for off in range(1, n_mp):
            attn_copy(off, g).wait()
        squares = jnp.zeros((rows, LANES), jnp.float32)
        for c in range(n_chunks):
            cols = slice(c * chunk, (c + 1) * chunk)
            total = acc[group_rows(g), cols]
            for off in range(1, n_mp):
                m = lax.rem(mp + off, n_mp)
                total = total + jnp.dot(
                    attn[m, group_rows(g), :], w[m, :, cols], preferred_element_type=jnp.float32
                )
            stored = (hidden[group_rows(g), cols].astype(jnp.float32) + total).astype(jnp.bfloat16)
            resid[:, cols] = stored
            v = stored.astype(jnp.float32)
            for i in range(chunk // LANES):
                piece = v[:, i * LANES : (i + 1) * LANES]
                squares = squares + piece * piece
        heads = lax.dot_general(
            heads_w[...], resid[...], (((1,), (1,)), ((), ())), preferred_element_type=jnp.float32
        )
        h = head_count
        part[mp, g, 0:h, :] = heads[0:h] + heads[h : 2 * h] + heads[2 * h : 3 * h]
        sum_row = jnp.sum(jnp.transpose(squares), axis=0, keepdims=True)
        part[mp, g, h : 2 * h, :] = jnp.broadcast_to(sum_row, (h, rows))
        for off in range(1, n_mp):
            part_copy(off, g).start()

        @pl.when(g > 0)
        def _():
            finish(g - 1)

        return carry

    lax.fori_loop(0, groups, second_half, 0)
    finish(groups - 1)

    seq_part = seq_acc[...]

    def fill(r, carry):
        send_buf[r, :, 0:block_len] = rewards[send_idx[r]]
        send_buf[r, :, block_len:] = seq_part
        return carry

    lax.fori_loop(0, n_dp, fill, 0, unroll=n_dp <= 16)
    recv_buf[dp] = send_buf[dp]
    for off in range(1, n_dp):
        dp_copy(off).start()
    for off in range(1, n_dp):
        dp_copy(off).wait()
    for q in range(OWN_CAP):
        rewards_out[q] = recv_buf[recv_idx[q], :, 0:block_len]
    totals = recv_buf[0, :, block_len:]
    for s in range(1, n_dp):
        totals = totals + recv_buf[s, :, block_len:]
    scores = totals[:, :seq_count] / len_v[...].reshape(1, seq_count).astype(jnp.float32)
    worst = jnp.min(scores, axis=0, keepdims=True)
    centred = scores - jnp.mean(scores, axis=0, keepdims=True)
    spread = jnp.mean(centred * centred, axis=0, keepdims=True)
    penalty_scale = jnp.mean(spread, axis=1, keepdims=True) + stat_epsilon
    conservative = worst - spread / penalty_scale
    shifted = conservative - jnp.mean(conservative, axis=1, keepdims=True)
    variance = jnp.mean(shifted * shifted, axis=1, keepdims=True)
    adv_buf[...] = jnp.zeros_like(adv_buf)
    adv_buf[0:1, :seq_count] = shifted * lax.rsqrt(variance + stat_epsilon)
    width = adv_buf.shape[1]
    seq_local = adv_out.shape[1]
    turned = pltpu.roll(adv_buf[...], width - dp * seq_local, 1)
    adv_out[...] = turned[0:1, :seq_local]


def local(n_dp, n_mp, hidden, attn_out, out_proj, norm_gain, reward_proj, block_seq, block_dest, lengths):
    slots, block_len, k_local = attn_out.shape
    n_local = out_proj.shape[1]
    seq_count = lengths.shape[0]
    seq_pad = -(-seq_count // LANES) * LANES
    heads = reward_proj.shape[1]
    per_group = split_size(slots)
    groups = slots // per_group
    rows = per_group * block_len
    total_rows = slots * block_len
    f32, bf16 = jnp.float32, jnp.bfloat16
    dma = pltpu.SemaphoreType.DMA
    any_spec = pl.BlockSpec(memory_space=pl.ANY)
    vmem_spec = pl.BlockSpec(memory_space=pltpu.VMEM)
    smem_spec = pl.BlockSpec(memory_space=pltpu.SMEM)
    token_rewards, advantages = pl.pallas_call(
        functools.partial(kernel, n_dp, n_mp, slots, block_len, seq_count, per_group),
        out_shape=(
            jax.ShapeDtypeStruct((OWN_CAP, heads, block_len), f32),
            jax.ShapeDtypeStruct((1, seq_count // n_dp), f32),
        ),
        in_specs=[any_spec] * 3 + [vmem_spec] * 2 + [smem_spec] * 3 + [vmem_spec] * 3,
        out_specs=(vmem_spec, vmem_spec),
        scratch_shapes=[
            pltpu.VMEM((n_mp, total_rows, k_local), bf16),
            pltpu.VMEM((n_mp, k_local, n_local), bf16),
            pltpu.VMEM((total_rows, n_local), bf16),
            pltpu.VMEM((total_rows, n_local), f32),
            pltpu.VMEM((rows, n_local), bf16),
            pltpu.VMEM((4 * heads, n_local), bf16),
            pltpu.VMEM((n_mp, groups, 2 * heads, rows), f32),
            pltpu.VMEM((slots + (-slots) % 8, block_len), f32),
            pltpu.VMEM((slots, heads, block_len), f32),
            pltpu.VMEM((heads, seq_pad), f32),
            pltpu.VMEM((n_dp, heads, block_len + seq_pad), f32),
            pltpu.VMEM((n_dp, heads, block_len + seq_pad), f32),
            pltpu.VMEM((8, seq_pad), f32),
            pltpu.SMEM((n_dp,), jnp.int32),
            pltpu.SMEM((OWN_CAP,), jnp.int32),
            dma((n_mp,)),
            dma((groups,)),
            dma((groups,)),
            dma((n_mp - 1, groups)),
            dma((n_mp - 1, groups)),
            dma((n_mp - 1, groups)),
            dma((n_mp - 1, groups)),
            dma((n_dp - 1,)),
            dma((n_dp - 1,)),
        ],
        compiler_params=pltpu.CompilerParams(
            collective_id=0, has_side_effects=True, vmem_limit_bytes=60 * 1024 * 1024
        ),
    )(
        hidden.reshape(total_rows, n_local),
        attn_out.reshape(total_rows, k_local),
        out_proj,
        norm_gain,
        reward_proj.T,
        block_seq,
        block_dest,
        lengths,
        block_seq,
        block_dest,
        lengths,
    )
    return token_rewards, advantages.reshape(seq_count // n_dp)


def solution(mesh):
    return jax.shard_map(
        functools.partial(local, mesh.shape["dp"], mesh.shape["mp"]),
        mesh=mesh,
        in_specs=(
            P("dp", None, "mp"),
            P("dp", None, "mp"),
            P(None, "mp"),
            P("mp"),
            P("mp", None),
            P(),
            P(),
            P(),
        ),
        out_specs=(P("dp", None, None), P("dp")),
        check_vma=False,
    )
```

time: 288 us -> 29.9 us (0.10)
  blocking collectives: 130 us -> 0 us
  waiting for transfers between devices: 102 us -> 0 us
  Pallas kernels: 0 us -> 26.5 us
  between operations: 18.6 us -> 0.64 us
  matrix products: 17.7 us -> 0 us
  starting transfers between devices: 7.03 us -> 0 us
  local copies, waits for them, and re-layouts: 7.81 us -> 2.54 us
  other arithmetic: 4.79 us -> 0 us
    unnamed x1 -> x0, blocking collectives: 89 us -> none
    all_to_all x1 -> x0, waiting for transfers between devices: 78.5 us -> none  [local(): lax.all_to_all(jnp.einsum('rj,jtf->rtf', selector, local_resid, preferred...]
    psum x2 -> x0, blocking collectives: 40.8 us -> none  [the longest x1 37.3 us: local(): lax.psum((jnp.sum(spread), jnp.sum(worst_case), jnp.sum(worst_case * wors...]
    pallas_call x0 -> x1, Pallas kernels: none -> 26.5 us  [local(): pl.pallas_call(functools.partial(kernel, n_dp, n_mp, slots, block_len, se...]
    all_gather x1 -> x0, waiting for transfers between devices: 22.5 us -> none  [local(): lax.all_gather(attn_out, 'mp', axis=2, tiled=True)]
    dot_general x4 -> x0, matrix products: 17.7 us -> none  [the longest x1 12.5 us: local(): jnp.einsum('btf,fc->btc', lax.all_gather(attn_out, 'mp', axis=2, tiled=Tr...]
    all_to_all x1 -> x0, starting transfers between devices: 6.99 us -> none  [local(): lax.all_to_all(jnp.einsum('rj,jtf->rtf', selector, local_resid, preferred...]
    convert_element_type x1 -> x0, local copies, waits for them, and re-layouts: 4.3 us -> none  [local(): jnp.einsum('rj,jtf->rtf', selector, local_resid, preferred_element_type=j...]
  transfers between devices with their start and end apart: 2 -> 0, of which waited for: 2 -> 0; matrix products, arithmetic and copies ran while one was open for 1% -> 0% of each run, Pallas kernels for 0% -> 0%
where the time goes in v1:
time: 29.9 us; the launch traced here: 29.7 us
  Pallas kernels  26.5 us (89%)
  local copies, waits for them, and re-layouts  2.54 us (8%)
  between operations  0.64 us (2%)
    pallas_call x1, Pallas kernels, local(): pl.pallas_call(functools.partial(kernel, n_dp, n_mp, slots, block_len, se...  26.5 us
    unnamed x2, local copies, waits for them, and re-layouts  2.54 us

profile of v1, /device:TPU:0, one launch (start us, length us, event | category | flops | bytes accessed | tf_op | source)
XLA Modules:
  0.0 29.7 jit_solution(11010976959441202424)
XLA Ops:
  0.6 26.5 %shard_map.95 = (f32[10,8,128]{2,1,0:T(8,128)}, f32[1,6]{1,0:T(1,128)}) custom-call(bf16[1920,1024]{1,0:T(8,128)(2,1)} %bitcast.4, bf16[1920,1024]{1,0:T(8,128)(2,1)} %bitcast.5, bf16[2048,1024]{1,0:T(8,128)(2,1)} %w_hbm.1, f32[1024]{0:T(1024)} %gain_ref.1, f32[8,1024]{1,0:T(8,128)} %bitcast.6, s32[240]{0:T(256)} %seq_v.1, s32[240]{0:T(256)} %dest_v.1, ...), custom_call_target="tpu_custom_call" | custom-call | tf_op jit(solution)/shard_map/pallas_call | solution.py:262
  27.1 1.4 %copy.12 = f32[10,8,128]{2,1,0:T(8,128)} copy(f32[10,8,128]{2,1,0:T(8,128)} %get-tuple-element.8) | data formatting | bytes 81920
  28.5 1.1 %copy.13 = f32[6]{0:T(128)} copy(f32[6]{0:T(128)} %bitcast.7) | data formatting | bytes 48

commit v2 on v1

--- a/solution.py
+++ b/solution.py
@@ -16,7 +16,7 @@
 
 
 def split_size(slots):
-    for size in (3, 4, 2, 5):
+    for size in (5, 4, 3, 2):
         if slots % size == 0:
             return size
     return 1
@@ -24,10 +24,10 @@
 
 def kernel(
     n_dp, n_mp, slots, block_len, seq_count, per_group,
-    hidden_hbm, attn_hbm, w_hbm, gain_ref, reward_ref, seq_s, dest_s, len_s, seq_v, dest_v, len_v,
-    rewards_out, adv_out,
-    attn, w, hidden, acc, resid, heads_w, part, live, rewards, seq_acc, send_buf, recv_buf, adv_buf,
-    send_idx, recv_idx,
+    hidden_hbm, attn_hbm, w_hbm, gain_hbm, reward_hbm, seq_hbm, dest_hbm, len_hbm,
+    recv_buf,
+    attn, w, hidden, acc, resid, heads_w, part, live, rewards, seq_acc, send_buf,
+    send_idx, gain_ref, reward_ref, seq_s, dest_s, len_s, seq_v, small_sem,
     w_sem, own_sem, hid_sem, attn_send, attn_recv, part_send, part_recv, dp_send, dp_recv,
 ):
     dp = lax.axis_index("dp")
@@ -90,6 +90,21 @@
             device_id_type=MESH,
         )
 
+    small = [
+        pltpu.make_async_copy(src, dst, small_sem.at[i])
+        for i, (src, dst) in enumerate(
+            (
+                (gain_hbm, gain_ref),
+                (reward_hbm, reward_ref),
+                (seq_hbm, seq_s),
+                (dest_hbm, dest_s),
+                (len_hbm, len_s),
+                (seq_hbm, seq_v),
+            )
+        )
+    ]
+    for copy in small:
+        copy.start()
     w_copy(mp).start()
     for g in range(groups):
         own_copy(g).start()
@@ -98,6 +113,8 @@
     for g in range(groups):
         hid_copy(g).start()
 
+    for copy in small:
+        copy.wait()
     head_count = reward_ref.shape[0]
     weighted = reward_ref[...] * gain_ref[...].reshape(1, n_local)
     high = weighted.astype(jnp.bfloat16)
@@ -120,11 +137,7 @@
     lax.fori_loop(0, n_dp, send_body, 0)
     all_slots = seq_s.shape[0]
     slot_lane = lax.broadcasted_iota(jnp.int32, (1, all_slots), 1)
-    dest_row = dest_v[...].reshape(1, all_slots)
     seq_row = seq_v[...].reshape(1, all_slots)
-    for q in range(OWN_CAP):
-        place = jnp.max(jnp.where(dest_row == dp * OWN_CAP + q, slot_lane, 0))
-        recv_idx[q] = lax.div(place, slots)
     token = lax.broadcasted_iota(jnp.int32, (1, block_len), 1).astype(jnp.float32)
     for j in range(slots):
         seq = seq_s[base + j]
@@ -218,13 +231,23 @@
         return carry
 
     lax.fori_loop(0, n_dp, fill, 0, unroll=n_dp <= 16)
-    recv_buf[dp] = send_buf[dp]
+    kept = pltpu.make_async_copy(send_buf.at[dp], recv_buf.at[dp], small_sem.at[0])
+    kept.start()
     for off in range(1, n_dp):
         dp_copy(off).start()
     for off in range(1, n_dp):
         dp_copy(off).wait()
+    kept.wait()
+
+
+def finish_kernel(n_dp, slots, seq_count, block_len, recv_buf, dest_v, len_v, rewards_out, adv_out, adv_buf):
+    dp = lax.axis_index("dp")
+    all_slots = dest_v.shape[0]
+    slot_lane = lax.broadcasted_iota(jnp.int32, (1, all_slots), 1)
+    dest_row = dest_v[...].reshape(1, all_slots)
     for q in range(OWN_CAP):
-        rewards_out[q] = recv_buf[recv_idx[q], :, 0:block_len]
+        place = jnp.max(jnp.where(dest_row == dp * OWN_CAP + q, slot_lane, 0))
+        rewards_out[q] = recv_buf[lax.div(place, slots), :, 0:block_len]
     totals = recv_buf[0, :, block_len:]
     for s in range(1, n_dp):
         totals = totals + recv_buf[s, :, block_len:]
@@ -243,7 +266,6 @@
     turned = pltpu.roll(adv_buf[...], width - dp * seq_local, 1)
     adv_out[...] = turned[0:1, :seq_local]
 
-
 def local(n_dp, n_mp, hidden, attn_out, out_proj, norm_gain, reward_proj, block_seq, block_dest, lengths):
     slots, block_len, k_local = attn_out.shape
     n_local = out_proj.shape[1]
@@ -258,15 +280,12 @@
     dma = pltpu.SemaphoreType.DMA
     any_spec = pl.BlockSpec(memory_space=pl.ANY)
     vmem_spec = pl.BlockSpec(memory_space=pltpu.VMEM)
-    smem_spec = pl.BlockSpec(memory_space=pltpu.SMEM)
-    token_rewards, advantages = pl.pallas_call(
+    width = block_len + seq_pad
+    received = pl.pallas_call(
         functools.partial(kernel, n_dp, n_mp, slots, block_len, seq_count, per_group),
-        out_shape=(
-            jax.ShapeDtypeStruct((OWN_CAP, heads, block_len), f32),
-            jax.ShapeDtypeStruct((1, seq_count // n_dp), f32),
-        ),
-        in_specs=[any_spec] * 3 + [vmem_spec] * 2 + [smem_spec] * 3 + [vmem_spec] * 3,
-        out_specs=(vmem_spec, vmem_spec),
+        out_shape=jax.ShapeDtypeStruct((n_dp, heads, width), f32),
+        in_specs=[any_spec] * 8,
+        out_specs=any_spec,
         scratch_shapes=[
             pltpu.VMEM((n_mp, total_rows, k_local), bf16),
             pltpu.VMEM((n_mp, k_local, n_local), bf16),
@@ -278,11 +297,15 @@
             pltpu.VMEM((slots + (-slots) % 8, block_len), f32),
             pltpu.VMEM((slots, heads, block_len), f32),
             pltpu.VMEM((heads, seq_pad), f32),
-            pltpu.VMEM((n_dp, heads, block_len + seq_pad), f32),
-            pltpu.VMEM((n_dp, heads, block_len + seq_pad), f32),
-            pltpu.VMEM((8, seq_pad), f32),
+            pltpu.VMEM((n_dp, heads, width), f32),
             pltpu.SMEM((n_dp,), jnp.int32),
-            pltpu.SMEM((OWN_CAP,), jnp.int32),
+            pltpu.VMEM(norm_gain.shape, f32),
+            pltpu.VMEM((heads, n_local), f32),
+            pltpu.SMEM(block_seq.shape, jnp.int32),
+            pltpu.SMEM(block_dest.shape, jnp.int32),
+            pltpu.SMEM(lengths.shape, jnp.int32),
+            pltpu.VMEM(block_seq.shape, jnp.int32),
+            dma((6,)),
             dma((n_mp,)),
             dma((groups,)),
             dma((groups,)),
@@ -305,10 +328,17 @@
         block_seq,
         block_dest,
         lengths,
-        block_seq,
-        block_dest,
-        lengths,
     )
+    token_rewards, advantages = pl.pallas_call(
+        functools.partial(finish_kernel, n_dp, slots, seq_count, block_len),
+        out_shape=(
+            jax.ShapeDtypeStruct((OWN_CAP, heads, block_len), f32),
+            jax.ShapeDtypeStruct((1, seq_count // n_dp), f32),
+        ),
+        in_specs=[vmem_spec] * 3,
+        out_specs=(vmem_spec, vmem_spec),
+        scratch_shapes=[pltpu.VMEM((8, seq_pad), f32)],
+    )(received, block_dest, lengths)
     return token_rewards, advantages.reshape(seq_count // n_dp)
 
 

time: 29.9 us -> 26.9 us (0.90)
  local copies, waits for them, and re-layouts: 2.54 us -> 0 us
  Pallas kernels: 26.5 us -> 26.1 us
    unnamed x2 -> x0, local copies, waits for them, and re-layouts: 2.54 us -> none
    pallas_call x1, Pallas kernels: 26.5 us -> 24.2 us  [local(): pl.pallas_call(functools.partial(kernel, n_dp, n_mp, slots, block_len, se...]
    pallas_call x0 -> x1, Pallas kernels: none -> 1.89 us  [local(): pl.pallas_call(functools.partial(finish_kernel, n_dp, slots, seq_count, b...]
where the time goes in v2:
time: 26.9 us; the launch traced here: 26.7 us
  Pallas kernels  26.1 us (97%)
  between operations  0.64 us (2%)
    pallas_call x1, Pallas kernels, local(): pl.pallas_call(functools.partial(kernel, n_dp, n_mp, slots, block_len, se...  24.2 us
    pallas_call x1, Pallas kernels, local(): pl.pallas_call(functools.partial(finish_kernel, n_dp, slots, seq_count, b...  1.89 us

profile of v2, /device:TPU:0, one launch (start us, length us, event | category | flops | bytes accessed | tf_op | source)
XLA Modules:
  0.0 26.7 jit_solution(14141650369470893897)
XLA Ops:
  0.6 24.2 %shard_map.95.recv_buf = f32[16,8,256]{2,1,0:T(8,128)} custom-call(bf16[1920,1024]{1,0:T(8,128)(2,1)} %bitcast.4, bf16[1920,1024]{1,0:T(8,128)(2,1)} %bitcast.5, bf16[2048,1024]{1,0:T(8,128)(2,1)} %w_hbm.1, f32[1024]{0:T(1024)} %gain_hbm.1, f32[8,1024]{1,0:T(8,128)} %bitcast.6, s32[240]{0:T(256)} %seq_hbm.1, s32[240]{0:T(256)} %dest_v.1, s32[96]{0:T(128)} %len_v.1), custom_call_target="tpu_custom_call" | custom-call | tf_op jit(solution)/shard_map/pallas_call | solution.py:284
  24.8 1.9 %shard_map.96 = (f32[10,8,128]{2,1,0:T(8,128)}, f32[1,6]{1,0:T(1,128)}) custom-call(f32[16,8,256]{2,1,0:T(8,128)} %shard_map.95.recv_buf, s32[240]{0:T(256)} %dest_v.1, s32[96]{0:T(128)} %len_v.1), custom_call_target="tpu_custom_call" | custom-call | tf_op jit(solution)/shard_map/pallas_call | solution.py:332
